TPU v7x, 128 devices: a whole 4x4x4 slice. The times are simulated.
128 devices in a mesh: row: 16 (over y, z), col: 8 (over x, core).
Axes of the slice: x: 4, y: 4, z: 4, core: 2. Of those that a mesh axis runs over, the one named last changes fastest.
Arguments:
- densities: bfloat16 [18432, 3072], P(('row', 'col')), may hold values from -0.796875 to 0.796875
- counts: int32 [2048], P(('row', 'col')), may hold values from 3 to 9
- coulomb: float32 [3072], replicated, may hold values from 0.05 to 1
- energies: float32 [18432], P(('row', 'col')), may hold values from 8 to 64
- vectors: bfloat16 [18432, 64], P(('row', 'col')), may hold values from -0.046875 to 0.046875
Outputs:
- kernel: float32 [18432, 18432], P('row', 'col')
- product: float32 [18432, 64], P(('row', 'col'))
All inputs are finite; a program needn't handle non-finite values.
Results may differ from a plain program's by a relative error of at most 0.0095.
Values may be sent and summed in bfloat16 or wider, within the bound.
No kernel may reach another device: no remote copies, remote signals or barrier semaphores. Data moves between devices by JAX's collectives and lax.ppermute only.
A program may use at most 128 MiB of HBM per device.

v0:
```python
import jax
import jax.numpy as jnp
from jax import lax
from jax.sharding import Mesh
from jax.sharding import PartitionSpec as P

SLOT = 9
ROW = ("row_0", "row_1")
ROW_COL = ("row_0", "row_1", "col")


def gather_axes(value, axes, dim):
    filled = value
    for number in range(len(axes) - 1, -1, -1):
        filled = lax.all_gather(filled, axes[number], axis=dim, tiled=True)
    return filled


def split_up(value, dim, count):
    before, after = (value.shape[:dim], value.shape[dim + 1 :])
    return jnp.moveaxis(value.reshape(*before, count, -1, *after), dim, 0)


def sent_and_summed(value, axis, dim):
    count = lax.axis_size(axis)
    blocks = lax.all_to_all(split_up(value, dim, count), axis, 0, 0, tiled=True)
    return jnp.sum(blocks.astype(jnp.float32), axis=0)


def split_product(matrix, right_side):
    high = matrix.astype(jnp.bfloat16)
    rest = matrix - high.astype(jnp.float32)
    middle = rest.astype(jnp.bfloat16)
    lowest = (rest - middle.astype(jnp.float32)).astype(jnp.bfloat16)
    total = jnp.dot(high, right_side, preferred_element_type=jnp.float32)
    total = total + jnp.dot(middle, right_side, preferred_element_type=jnp.float32)
    return total + jnp.dot(lowest, right_side, preferred_element_type=jnp.float32)


def body(densities, counts, coulomb, energies, vectors):
    kpoints = counts.shape[0]
    slot_index = lax.broadcasted_iota(jnp.int32, (kpoints, SLOT), 1)
    usable = (slot_index < counts[:, None]).reshape(kpoints * SLOT)
    masked = jnp.where(usable[:, None], densities, jnp.zeros_like(densities))
    weighted = (masked.astype(jnp.float32) * coulomb[None, :]).astype(jnp.bfloat16)
    row_block = lax.all_gather(weighted, "col", axis=0, tiled=True)
    kernel = lax.dot_general(
        row_block,
        lax.all_gather(masked, ROW, axis=0, tiled=True),
        (((1,), (1,)), ((), ())),
        preferred_element_type=jnp.float32,
    )
    column_vectors = gather_axes(vectors, ROW, 0)
    partial_value = split_product(kernel, column_vectors)
    coupled = sent_and_summed(partial_value.astype(jnp.bfloat16), "col", 0)
    diagonal = jnp.where(usable, energies, jnp.zeros_like(energies))
    product = coupled + diagonal[:, None] * vectors.astype(jnp.float32)
    return (kernel, product)


def solution(mesh):
    finer = Mesh(mesh.devices.reshape(4, 4, mesh.shape["col"]), ("row_0", "row_1", "col"))
    in_specs = (P(ROW_COL, None), P(ROW_COL), P(), P(ROW_COL), P(ROW_COL, None))
    out_specs = (P(ROW, "col"), P(ROW_COL, None))
    return jax.shard_map(body, mesh=finer, in_specs=in_specs, out_specs=out_specs, check_vma=False)
```

profile of v0, /device:TPU:1, one launch (start us, length us, event | category | flops | bytes accessed | tf_op | source)
XLA Modules:
  0.0 206.2 jit_solution(9412224943959909971)
XLA Ops:
  7.2 0.0 all-gather.5.cloned.1.call-start
  7.2 0.7 iota_compare_fusion
  7.9 0.1 lt.18
  8.0 2.8 %multiply_convert_fusion = (bf16[144,3072]{1,0:T(8,128)(2,1)}, bf16[144,3072]{1,0:T(8,128)(2,1)}) fusion(f32[3072]{0:T(1024)} %param.7, bf16[144,3072]{1,0:T(8,128)(2,1)} %param.5, pred[144]{0:T(512)(128)(4,1)S(1)} %lt.18), kind=kLoop, calls=%fused_computation.10 | loop fusion | flops 1769472 | bytes 2666640 | tf_op jit(solution)/shard_map/convert_element_type | solution.py:45
  10.8 0.0 all-gather.5.cloned.1.call-update
  10.8 0.0 all-gather.7.cloned.1.call-start
  10.9 0.7 all-gather.7.cloned.1.call-update
  11.6 11.8 %all-gather = bf16[4,144,64]{1,2,0:T(8,128)(2,1)S(1)} all-gather(bf16[1,144,64]{1,2,0:T(8,128)(2,1)} %bitcast.12), channel_id=1, replica_groups=mesh['row_0'=4,'row_1'=4,'col'=8] {'row_1'}, dimensions={0}, use_global_device_ids=true | all-gather | bytes 92160 | tf_op jit(solution)/shard_map/all_gather | solution.py:15
  23.4 0.1 copy.10
  23.5 0.1 reshape.30
  23.6 11.2 %all-gather.1 = bf16[4,576,64]{1,2,0:T(8,128)(2,1)S(1)} all-gather(bf16[1,576,64]{1,2,0:T(8,128)(2,1)S(1)} %reshape.30), channel_id=1, replica_groups=mesh['row_0'=4,'row_1'=4,'col'=8] {'row_0'}, dimensions={0}, use_global_device_ids=true | all-gather | bytes 368640 | tf_op jit(solution)/shard_map/all_gather | solution.py:15
  34.9 0.3 copy.11
  35.1 0.3 reshape.31
  35.4 23.3 %all-gather.5.cloned.1.call-done = bf16[1152,3072]{1,0:T(8,128)(2,1)} async-done(((bf16[144,3072]{1,0:T(8,128)(2,1)}), bf16[1152,3072]{1,0:T(8,128)(2,1)}) %all-gather.5.cloned.1.call-update) | async-done | bytes 7077904 | tf_op jit(solution)/shard_map/all_gather | solution.py:46
  58.7 99.7 %all-gather.7.cloned.1.call-done = bf16[2304,3072]{1,0:T(8,128)(2,1)} async-done(((bf16[144,3072]{1,0:T(8,128)(2,1)}), bf16[2304,3072]{1,0:T(8,128)(2,1)}) %all-gather.7.cloned.1.call-update) | async-done | bytes 14155792 | tf_op jit(solution)/shard_map/all_gather | solution.py:49
  158.4 21.7 %fusion.11 = f32[1152,2304]{1,0:T(8,128)S(1)} fusion(bf16[1152,3072]{1,0:T(8,128)(2,1)} %all-gather.5.cloned.1.call-done, bf16[2304,3072]{1,0:T(8,128)(2,1)} %all-gather.7.cloned.1.call-done), kind=kOutput, calls=%fused_computation.16 | convolution fusion | flops 16307453952 | bytes 31850496 | tf_op jit(solution)/shard_map/dot_general | solution.py:47
  180.1 0.0 copy-start
  180.1 1.7 fusion.1
  181.9 1.8 fusion.7
  183.6 0.6 copy-done
  184.2 0.0 copy-start.2
  184.2 0.0 copy-start.1
  184.2 1.8 fusion.10
  186.0 0.4 reshape.27
  186.4 0.7 copy.12
  187.1 5.1 %all-to-all-start = ((bf16[8,144,64]{1,2,0:T(8,128)(2,1)}), bf16[8,144,64]{1,2,0:T(8,128)(2,1)S(1)}, u32[]{:S(2)}, u32[]{:S(2)}) async-start(bf16[8,144,64]{1,2,0:T(8,128)(2,1)} %copy.12), calls=%async_computation | async-start | bytes 524288 | tf_op jit(solution)/shard_map/all_to_all | solution.py:26
  192.2 0.0 copy-done.2
  192.2 6.5 %all-to-all-done = bf16[8,144,64]{1,2,0:T(8,128)(2,1)S(1)} async-done(((bf16[8,144,64]{1,2,0:T(8,128)(2,1)}), bf16[8,144,64]{1,2,0:T(8,128)(2,1)S(1)}, u32[]{:S(2)}, u32[]{:S(2)}) %all-to-all-start) | async-done | bytes 147488 | tf_op jit(solution)/shard_map/all_to_all | solution.py:26
  198.8 0.0 copy-done.1
  198.8 0.6 multiply_add_fusion
  (2 shorter events, 0.1 us)
Async XLA Ops:
  7.2 51.6 %all-gather.5.cloned.1.call-start = ((), (), s32[]{:S(2)}) async-start(), calls=%async_computation.1 | async-start | bytes 7962624 | tf_op jit(solution)/shard_map/all_gather | solution.py:46
  10.8 147.6 %all-gather.7.cloned.1.call-start = ((), (), s32[]{:S(2)}) async-start(), calls=%async_computation.2 | async-start | bytes 15040512 | tf_op jit(solution)/shard_map/all_gather | solution.py:49
  180.1 4.1 %copy-start = (f32[1152,2304]{1,0:T(8,128)}, f32[1152,2304]{1,0:T(8,128)S(1)}, u32[]{:S(2)}) copy-start(f32[1152,2304]{1,0:T(8,128)S(1)} %fusion.11) | copy-start | bytes 31850500
  184.2 8.0 %copy-start.2 = (f32[144]{0:T(256)S(1)}, f32[144]{0:T(256)}, u32[]{:S(2)}) copy-start(f32[144]{0:T(256)} %param.8) | copy-start | bytes 1732
  184.2 14.5 %copy-start.1 = (bf16[144,64]{0,1:T(8,128)(2,1)S(1)}, bf16[144,64]{0,1:T(8,128)(2,1)}, u32[]{:S(2)}) copy-start(bf16[144,64]{0,1:T(8,128)(2,1)} %param.9) | copy-start | bytes 55300
  187.1 11.6 %all-to-all-start = ((bf16[8,144,64]{1,2,0:T(8,128)(2,1)}), bf16[8,144,64]{1,2,0:T(8,128)(2,1)S(1)}, u32[]{:S(2)}, u32[]{:S(2)}) async-start(bf16[8,144,64]{1,2,0:T(8,128)(2,1)} %copy.12), calls=%async_computation | async-start | bytes 524288 | tf_op jit(solution)/shard_map/all_to_all | solution.py:26
Sparse Core Ops, SparseCore 0:
  11.0 47.7 all-gather.4
  60.9 97.4 all-gather.6
where the time goes:
time: 207 us; the launch traced here: 206 us
  waiting for transfers between devices  130 us (63%)
  matrix products  27 us (13%)
  blocking collectives  23 us (11%)
  between operations  14.1 us (7%)
  starting transfers between devices  5.17 us (2%)
  other arithmetic  4.2 us (2%)
  local copies, waits for them, and re-layouts  2.6 us (1%)
    all_gather x1, waiting for transfers between devices, body(): lax.all_gather(masked, ROW, axis=0, tiled=True)  99.7 us
    all_gather x1, waiting for transfers between devices, body(): row_block = lax.all_gather(weighted, 'col', axis=0, tiled=True)  23.3 us
    all_gather x2, blocking collectives, gather_axes(): filled = lax.all_gather(filled, axes[number], axis=dim, tiled=True)  23 us
    dot_general x1, matrix products, body(): lax.dot_general(row_block, lax.all_gather(masked, ROW, axis=0, tiled=True...  21.7 us
    all_to_all x1, waiting for transfers between devices, sent_and_summed(): blocks = lax.all_to_all(split_up(value, dim, count), axis, 0, 0, tiled=True)  6.46 us
    all_to_all x1, starting transfers between devices, sent_and_summed(): blocks = lax.all_to_all(split_up(value, dim, count), axis, 0, 0, tiled=True)  5.09 us
  transfers between devices with their start and end apart: 3, of which 3 were waited for; matrix products, arithmetic and copies ran while one was open for 0% of the time, Pallas kernels for 0%

commit v1 on v0

--- a/solution.py
+++ b/solution.py
@@ -43,7 +43,25 @@
     usable = (slot_index < counts[:, None]).reshape(kpoints * SLOT)
     masked = jnp.where(usable[:, None], densities, jnp.zeros_like(densities))
     weighted = (masked.astype(jnp.float32) * coulomb[None, :]).astype(jnp.bfloat16)
-    row_block = lax.all_gather(weighted, "col", axis=0, tiled=True)
+    peers, here, rows = (lax.axis_size("col"), lax.axis_index("col"), weighted.shape[0])
+    right = [(i, (i + 1) % peers) for i in range(peers)]
+    left = [(i, (i - 1) % peers) for i in range(peers)]
+    row_block = jnp.zeros(
+        (*weighted.shape[:0], peers * rows, *weighted.shape[0 + 1 :]), weighted.dtype
+    )
+    row_block = lax.dynamic_update_slice_in_dim(row_block, weighted, here * rows, axis=0)
+    from_left = from_right = weighted
+    middle_2 = peers // 2
+    for step in range(1, middle_2 + 1):
+        from_left = lax.ppermute(from_left, "col", right)
+        row_block = lax.dynamic_update_slice_in_dim(
+            row_block, from_left, (here - step) % peers * rows, axis=0
+        )
+        if step < peers - middle_2:
+            from_right = lax.ppermute(from_right, "col", left)
+            row_block = lax.dynamic_update_slice_in_dim(
+                row_block, from_right, (here + step) % peers * rows, axis=0
+            )
     kernel = lax.dot_general(
         row_block,
         lax.all_gather(masked, ROW, axis=0, tiled=True),

time: 207 us -> 164 us (0.79)
  waiting for transfers between devices: 130 us -> 61.8 us
  starting transfers between devices: 5.17 us -> 19.6 us
  local copies, waits for them, and re-layouts: 2.6 us -> 14.4 us
    all_gather x1, waiting for transfers between devices: 99.7 us -> 33.7 us  [body(): lax.all_gather(masked, ROW, axis=0, tiled=True)]
    all_gather x1 -> x0, waiting for transfers between devices: 23.3 us -> none  [body(): row_block = lax.all_gather(weighted, 'col', axis=0, tiled=True)]
    ppermute x0 -> x7, waiting for transfers between devices: none -> 21.6 us  [the longest x4 20.1 us: body(): from_left = lax.ppermute(from_left, 'col', right)]
    ppermute x0 -> x7, starting transfers between devices: none -> 14.8 us  [the longest x4 13.4 us: body(): from_left = lax.ppermute(from_left, 'col', right)]
    dynamic_update_slice x0 -> x7, local copies, waits for them, and re-layouts: none -> 7.94 us  [the longest x4 5.04 us: body(): lax.dynamic_update_slice_in_dim(row_block, from_left, (here - step) % pee...]
    broadcast_in_dim x0 -> x1, local copies, waits for them, and re-layouts: none -> 3.85 us  [body(): jnp.zeros((*weighted.shape[:0], peers * rows, *weighted.shape[0 + 1:]), w...]
    convert_element_type x1 -> x0, other arithmetic: 2.78 us -> none  [body(): (masked.astype(jnp.float32) * coulomb[None, :]).astype(jnp.bfloat16)]
  transfers between devices with their start and end apart: 3 -> 9, of which waited for: 3 -> 6; matrix products, arithmetic and copies ran while one was open for 0% -> 5% of each run, Pallas kernels for 0% -> 0%
where the time goes in v1:
time: 164 us
  waiting for transfers between devices  61.8 us (38%)
  matrix products  27 us (16%)
  blocking collectives  23.6 us (14%)
  starting transfers between devices  19.6 us (12%)
  local copies, waits for them, and re-layouts  14.4 us (9%)
  between operations  14.2 us (9%)
  other arithmetic  3.16 us (2%)
    all_gather x1, waiting for transfers between devices, body(): lax.all_gather(masked, ROW, axis=0, tiled=True)  33.7 us
    all_gather x2, blocking collectives, gather_axes(): filled = lax.all_gather(filled, axes[number], axis=dim, tiled=True)  23.6 us
    dot_general x1, matrix products, body(): lax.dot_general(row_block, lax.all_gather(masked, ROW, axis=0, tiled=True...  21.7 us
    ppermute x4, waiting for transfers between devices, body(): from_left = lax.ppermute(from_left, 'col', right)  20.1 us
    ppermute x4, starting transfers between devices, body(): from_left = lax.ppermute(from_left, 'col', right)  13.4 us
    all_to_all x1, waiting for transfers between devices, sent_and_summed(): blocks = lax.all_to_all(split_up(value, dim, count), axis, 0, 0, tiled=True)  6.46 us
    dynamic_update_slice x4, local copies, waits for them, and re-layouts, body(): lax.dynamic_update_slice_in_dim(row_block, from_left, (here - step) % pee...  5.04 us
    all_to_all x1, starting transfers between devices, sent_and_summed(): blocks = lax.all_to_all(split_up(value, dim, count), axis, 0, 0, tiled=True)  4.75 us
  transfers between devices with their start and end apart: 9, of which 6 were waited for; matrix products, arithmetic and copies ran while one was open for 5% of the time, Pallas kernels for 0%

profile of v1, /device:TPU:1, one launch (start us, length us, event | category | flops | bytes accessed | tf_op | source)
XLA Modules:
  0.0 163.7 jit_solution(17550822412426189017)
XLA Ops:
  7.2 0.0 copy-start.1
  7.2 0.0 copy-start.3
  7.2 0.0 copy-start.2
  7.2 0.0 all-gather.4.cloned.1.call-start
  7.2 0.8 iota_compare_fusion
  8.0 0.1 lt.72
  8.1 3.9 %broadcast_in_dim.20 = bf16[1152,3072]{1,0:T(8,128)(2,1)} broadcast(bf16[]{:T(256)} %constant.52.clone.1), dimensions={} | broadcast | bytes 7077890 | tf_op jit(solution)/shard_map/broadcast_in_dim | solution.py:49
  12.0 0.0 copy-done.1
  12.0 0.0 copy-done.3
  12.0 1.7 %constant_dynamic-update-slice_fusion.7 = (bf16[1152,3072]{1,0:T(8,128)(2,1)}, bf16[144,3072]{1,0:T(8,128)(2,1)S(1)}, bf16[144,3072]{1,0:T(8,128)(2,1)}) fusion(bf16[1152,3072]{1,0:T(8,128)(2,1)} %broadcast_in_dim.20, s32[]{:T(128)S(6)} %select_n.64, f32[3072]{0:T(1024)S(1)} %copy-done.3, bf16[144,3072]{1,0:T(8,128)(2,1)S(1)} %copy-done.1, ...), kind=kLoop, calls=%fused_computation.22 | loop fusion | flops 1769472 | bytes 3551380 | tf_op jit(solution)/shard_map/dynamic_update_slice | solution.py:52
  13.7 0.0 all-gather.4.cloned.1.call-update
  13.7 2.6 %collective-permute-start = (bf16[144,3072]{1,0:T(8,128)(2,1)S(1)}, bf16[144,3072]{1,0:T(8,128)(2,1)}, u32[]{:S(2)}, u32[]{:S(2)}) collective-permute-start(bf16[144,3072]{1,0:T(8,128)(2,1)S(1)} %get-tuple-element.3), channel_id=1, source_target_pairs={{0,1},{1,2},{2,3},{3,4},{4,5},{5,6},{6,7},{7,0},{8,9},{9,10},{10,1... | collective-permute-start | bytes 2654216 | tf_op jit(solution)/shard_map/ppermute | solution.py:56
  16.3 0.0 collective-permute-start.1
  16.3 10.0 %collective-permute-done = bf16[144,3072]{1,0:T(8,128)(2,1)} collective-permute-done((bf16[144,3072]{1,0:T(8,128)(2,1)S(1)}, bf16[144,3072]{1,0:T(8,128)(2,1)}, u32[]{:S(2)}, u32[]{:S(2)}) %collective-permute-start) | collective-permute-done | bytes 884768 | tf_op jit(solution)/shard_map/ppermute | solution.py:56
  26.3 2.6 %collective-permute-start.2 = (bf16[144,3072]{1,0:T(8,128)(2,1)}, bf16[144,3072]{1,0:T(8,128)(2,1)S(1)}, u32[]{:S(2)}, u32[]{:S(2)}) collective-permute-start(bf16[144,3072]{1,0:T(8,128)(2,1)} %collective-permute-done), channel_id=1, source_target_pairs={{0,1},{1,2},{2,3},{3,4},{4,5},{5,6},{6,7},{7,0},{8,9},{9,10},{10,1... | collective-permute-start | bytes 2654216 | tf_op jit(solution)/shard_map/ppermute | solution.py:56
  28.9 0.0 collective-permute-done.1
  28.9 0.0 collective-permute-start.3
  28.9 0.0 copy-done.2
  28.9 12.3 %all-gather = bf16[4,144,64]{1,2,0:T(8,128)(2,1)S(1)} all-gather(bf16[1,144,64]{1,2,0:T(8,128)(2,1)S(1)} %bitcast.12), channel_id=1, replica_groups=mesh['row_0'=4,'row_1'=4,'col'=8] {'row_1'}, dimensions={0}, use_global_device_ids=true | all-gather | bytes 92160 | tf_op jit(solution)/shard_map/all_gather | solution.py:15
  41.2 0.1 copy.10
  41.3 0.1 reshape.30
  41.4 11.3 %all-gather.1 = bf16[4,576,64]{1,2,0:T(8,128)(2,1)S(1)} all-gather(bf16[1,576,64]{1,2,0:T(8,128)(2,1)S(1)} %reshape.30), channel_id=1, replica_groups=mesh['row_0'=4,'row_1'=4,'col'=8] {'row_0'}, dimensions={0}, use_global_device_ids=true | all-gather | bytes 368640 | tf_op jit(solution)/shard_map/all_gather | solution.py:15
  52.7 0.3 copy.11
  53.0 0.3 reshape.31
  53.3 0.0 collective-permute-done.2
  53.3 5.8 %collective-permute-start.4 = (bf16[144,3072]{1,0:T(8,128)(2,1)S(1)}, bf16[144,3072]{1,0:T(8,128)(2,1)S(1)}, u32[]{:S(2)}, u32[]{:S(2)}) collective-permute-start(bf16[144,3072]{1,0:T(8,128)(2,1)S(1)} %collective-permute-done.2), channel_id=1, source_target_pairs={{0,1},{1,2},{2,3},{3,4},{4,5},{5,6},{6,7},{7,0},{8,9},{9,10},{10,1... | collective-permute-start | bytes 2654216 | tf_op jit(solution)/shard_map/ppermute | solution.py:56
  59.1 2.1 %constant_dynamic-update-slice_fusion.6 = bf16[1152,3072]{1,0:T(8,128)(2,1)} fusion(bf16[1152,3072]{1,0:T(8,128)(2,1)} %get-tuple-element.2, bf16[144,3072]{1,0:T(8,128)(2,1)} %collective-permute-done, s32[]{:T(128)S(6)} %select_n.66), kind=kLoop, calls=%fused_computation.21 | loop fusion | bytes 1769476 | tf_op jit(solution)/shard_map/dynamic_update_slice | solution.py:57
  61.2 1.0 constant_dynamic-update-slice_fusion.5
  62.2 0.0 collective-permute-done.3
  62.2 1.4 collective-permute-start.5
  63.6 1.0 constant_dynamic-update-slice_fusion.4
  64.5 4.6 %collective-permute-done.4 = bf16[144,3072]{1,0:T(8,128)(2,1)S(1)} collective-permute-done((bf16[144,3072]{1,0:T(8,128)(2,1)S(1)}, bf16[144,3072]{1,0:T(8,128)(2,1)S(1)}, u32[]{:S(2)}, u32[]{:S(2)}) %collective-permute-start.4) | collective-permute-done | bytes 884768 | tf_op jit(solution)/shard_map/ppermute | solution.py:56
  69.1 2.5 %collective-permute-start.6 = (bf16[144,3072]{1,0:T(8,128)(2,1)S(1)}, bf16[144,3072]{1,0:T(8,128)(2,1)S(1)}, u32[]{:S(2)}, u32[]{:S(2)}) collective-permute-start(bf16[144,3072]{1,0:T(8,128)(2,1)S(1)} %collective-permute-done.4), channel_id=1, source_target_pairs={{0,1},{1,2},{2,3},{3,4},{4,5},{5,6},{6,7},{7,0},{8,9},{9,10},{10,1... | collective-permute-start | bytes 2654216 | tf_op jit(solution)/shard_map/ppermute | solution.py:56
  71.6 1.0 constant_dynamic-update-slice_fusion.3
  72.5 1.0 constant_dynamic-update-slice_fusion.2
  73.5 1.6 collective-permute-done.5
  75.1 1.0 constant_dynamic-update-slice_fusion.1
  76.0 5.5 %collective-permute-done.6 = bf16[144,3072]{1,0:T(8,128)(2,1)S(1)} collective-permute-done((bf16[144,3072]{1,0:T(8,128)(2,1)S(1)}, bf16[144,3072]{1,0:T(8,128)(2,1)S(1)}, u32[]{:S(2)}, u32[]{:S(2)}) %collective-permute-start.6) | collective-permute-done | bytes 884768 | tf_op jit(solution)/shard_map/ppermute | solution.py:56
  81.6 1.0 constant_dynamic-update-slice_fusion
  82.5 33.7 %all-gather.4.cloned.1.call-done = bf16[2304,3072]{1,0:T(8,128)(2,1)} async-done(((bf16[144,3072]{1,0:T(8,128)(2,1)}), bf16[2304,3072]{1,0:T(8,128)(2,1)}) %all-gather.4.cloned.1.call-update) | async-done | bytes 14155792 | tf_op jit(solution)/shard_map/all_gather | solution.py:67
  116.2 21.7 %fusion.11 = f32[1152,2304]{1,0:T(8,128)S(1)} fusion(bf16[1152,3072]{1,0:T(8,128)(2,1)} %constant_dynamic-update-slice_fusion, bf16[2304,3072]{1,0:T(8,128)(2,1)} %all-gather.4.cloned.1.call-done), kind=kOutput, calls=%fused_computation.24 | convolution fusion | flops 16307453952 | bytes 31850496 | tf_op jit(solution)/shard_map/dot_general | solution.py:65
  137.9 0.0 copy-start
  137.9 1.7 %fusion.1 = f32[1152,64]{0,1:T(8,128)S(1)} fusion(bf16[2304,64]{0,1:T(8,128)(2,1)S(1)} %reshape.31, f32[1152,2304]{1,0:T(8,128)S(1)} %fusion.11), kind=kOutput, calls=%fused_computation.3 | convolution fusion | flops 342392832 | bytes 11206656 | tf_op jit(solution)/shard_map/dot_general | solution.py:35
  139.6 1.8 %fusion.7 = f32[1152,64]{0,1:T(8,128)S(1)} fusion(f32[1152,64]{0,1:T(8,128)S(1)} %fusion.1, bf16[2304,64]{0,1:T(8,128)(2,1)S(1)} %reshape.31, f32[1152,2304]{1,0:T(8,128)S(1)} %fusion.11), kind=kOutput, calls=%fused_computation.8 | convolution fusion | flops 350429184 | bytes 11501568 | tf_op jit(solution)/shard_map/dot_general | solution.py:36
  141.4 0.6 copy-done
  142.0 0.0 copy-start.4
  142.0 1.8 %fusion.10 = bf16[1152,64]{0,1:T(8,128)(2,1)S(1)} fusion(f32[1152,64]{0,1:T(8,128)S(1)} %fusion.7, bf16[2304,64]{0,1:T(8,128)(2,1)S(1)} %reshape.31, f32[1152,2304]{1,0:T(8,128)S(1)} %fusion.11), kind=kOutput, calls=%fused_computation.9 | convolution fusion | flops 358465536 | bytes 11354112 | tf_op jit(solution)/shard_map/dot_general | solution.py:37
  143.8 0.4 reshape.27
  144.2 0.7 copy.12
  144.9 4.8 %all-to-all-start = ((bf16[8,144,64]{1,2,0:T(8,128)(2,1)}), bf16[8,144,64]{1,2,0:T(8,128)(2,1)S(1)}, u32[]{:S(2)}, u32[]{:S(2)}) async-start(bf16[8,144,64]{1,2,0:T(8,128)(2,1)} %copy.12), calls=%async_computation | async-start | bytes 524288 | tf_op jit(solution)/shard_map/all_to_all | solution.py:26
  149.7 0.0 copy-done.4
  149.7 6.5 %all-to-all-done = bf16[8,144,64]{1,2,0:T(8,128)(2,1)S(1)} async-done(((bf16[8,144,64]{1,2,0:T(8,128)(2,1)}), bf16[8,144,64]{1,2,0:T(8,128)(2,1)S(1)}, u32[]{:S(2)}, u32[]{:S(2)}) %all-to-all-start) | async-done | bytes 147488 | tf_op jit(solution)/shard_map/all_to_all | solution.py:26
  156.2 0.6 multiply_add_fusion
  (2 shorter events, 0.1 us)
Async XLA Ops:
  7.2 4.8 %copy-start.1 = (bf16[144,3072]{1,0:T(8,128)(2,1)S(1)}, bf16[144,3072]{1,0:T(8,128)(2,1)}, u32[]{:S(2)}) copy-start(bf16[144,3072]{1,0:T(8,128)(2,1)} %param.5) | copy-start | bytes 2654212
  7.2 4.8 %copy-start.3 = (f32[3072]{0:T(1024)S(1)}, f32[3072]{0:T(1024)}, u32[]{:S(2)}) copy-start(f32[3072]{0:T(1024)} %param.7) | copy-start | bytes 36868
  7.2 21.7 %copy-start.2 = (bf16[144,64]{0,1:T(8,128)(2,1)S(1)}, bf16[144,64]{0,1:T(8,128)(2,1)}, u32[]{:S(2)}) copy-start(bf16[144,64]{0,1:T(8,128)(2,1)} %param.9) | copy-start | bytes 55300
  7.2 109.0 %all-gather.4.cloned.1.call-start = ((), (), s32[]{:S(2)}) async-start(), calls=%async_computation.1 | async-start | bytes 15040512 | tf_op jit(solution)/shard_map/all_gather | solution.py:67
  13.7 12.6 %collective-permute-start = (bf16[144,3072]{1,0:T(8,128)(2,1)S(1)}, bf16[144,3072]{1,0:T(8,128)(2,1)}, u32[]{:S(2)}, u32[]{:S(2)}) collective-permute-start(bf16[144,3072]{1,0:T(8,128)(2,1)S(1)} %get-tuple-element.3), channel_id=1, source_target_pairs={{0,1},{1,2},{2,3},{3,4},{4,5},{5,6},{6,7},{7,0},{8,9},{9,10},{10,1... | collective-permute-start | bytes 2654216 | tf_op jit(solution)/shard_map/ppermute | solution.py:56
  16.3 12.6 %collective-permute-start.1 = (bf16[144,3072]{1,0:T(8,128)(2,1)S(1)}, bf16[144,3072]{1,0:T(8,128)(2,1)S(1)}, u32[]{:S(2)}, u32[]{:S(2)}) collective-permute-start(bf16[144,3072]{1,0:T(8,128)(2,1)S(1)} %get-tuple-element.3), channel_id=1, source_target_pairs={{0,7},{1,0},{2,1},{3,2},{4,3},{5,4},{6,5},{7,6},{8,15},{9,8},{10,9... | collective-permute-start | bytes 2654216 | tf_op jit(solution)/shard_map/ppermute | solution.py:61
  26.3 27.0 %collective-permute-start.2 = (bf16[144,3072]{1,0:T(8,128)(2,1)}, bf16[144,3072]{1,0:T(8,128)(2,1)S(1)}, u32[]{:S(2)}, u32[]{:S(2)}) collective-permute-start(bf16[144,3072]{1,0:T(8,128)(2,1)} %collective-permute-done), channel_id=1, source_target_pairs={{0,1},{1,2},{2,3},{3,4},{4,5},{5,6},{6,7},{7,0},{8,9},{9,10},{10,1... | collective-permute-start | bytes 2654216 | tf_op jit(solution)/shard_map/ppermute | solution.py:56
  28.9 33.3 %collective-permute-start.3 = (bf16[144,3072]{1,0:T(8,128)(2,1)S(1)}, bf16[144,3072]{1,0:T(8,128)(2,1)S(1)}, u32[]{:S(2)}, u32[]{:S(2)}) collective-permute-start(bf16[144,3072]{1,0:T(8,128)(2,1)S(1)} %collective-permute-done.1), channel_id=1, source_target_pairs={{0,7},{1,0},{2,1},{3,2},{4,3},{5,4},{6,5},{7,6},{8,15},{9,8},{10,9... | collective-permute-start | bytes 2654216 | tf_op jit(solution)/shard_map/ppermute | solution.py:61
  53.3 15.8 %collective-permute-start.4 = (bf16[144,3072]{1,0:T(8,128)(2,1)S(1)}, bf16[144,3072]{1,0:T(8,128)(2,1)S(1)}, u32[]{:S(2)}, u32[]{:S(2)}) collective-permute-start(bf16[144,3072]{1,0:T(8,128)(2,1)S(1)} %collective-permute-done.2), channel_id=1, source_target_pairs={{0,1},{1,2},{2,3},{3,4},{4,5},{5,6},{6,7},{7,0},{8,9},{9,10},{10,1... | collective-permute-start | bytes 2654216 | tf_op jit(solution)/shard_map/ppermute | solution.py:56
  62.2 12.9 %collective-permute-start.5 = (bf16[144,3072]{1,0:T(8,128)(2,1)S(1)}, bf16[144,3072]{1,0:T(8,128)(2,1)S(1)}, u32[]{:S(2)}, u32[]{:S(2)}) collective-permute-start(bf16[144,3072]{1,0:T(8,128)(2,1)S(1)} %collective-permute-done.3), channel_id=1, source_target_pairs={{0,7},{1,0},{2,1},{3,2},{4,3},{5,4},{6,5},{7,6},{8,15},{9,8},{10,9... | collective-permute-start | bytes 2654216 | tf_op jit(solution)/shard_map/ppermute | solution.py:61
  69.1 12.5 %collective-permute-start.6 = (bf16[144,3072]{1,0:T(8,128)(2,1)S(1)}, bf16[144,3072]{1,0:T(8,128)(2,1)S(1)}, u32[]{:S(2)}, u32[]{:S(2)}) collective-permute-start(bf16[144,3072]{1,0:T(8,128)(2,1)S(1)} %collective-permute-done.4), channel_id=1, source_target_pairs={{0,1},{1,2},{2,3},{3,4},{4,5},{5,6},{6,7},{7,0},{8,9},{9,10},{10,1... | collective-permute-start | bytes 2654216 | tf_op jit(solution)/shard_map/ppermute | solution.py:56
  137.9 4.1 %copy-start = (f32[1152,2304]{1,0:T(8,128)}, f32[1152,2304]{1,0:T(8,128)S(1)}, u32[]{:S(2)}) copy-start(f32[1152,2304]{1,0:T(8,128)S(1)} %fusion.11) | copy-start | bytes 31850500
  142.0 7.7 %copy-start.4 = (f32[144]{0:T(256)S(1)}, f32[144]{0:T(256)}, u32[]{:S(2)}) copy-start(f32[144]{0:T(256)} %param.8) | copy-start | bytes 1732
  144.9 11.2 %all-to-all-start = ((bf16[8,144,64]{1,2,0:T(8,128)(2,1)}), bf16[8,144,64]{1,2,0:T(8,128)(2,1)S(1)}, u32[]{:S(2)}, u32[]{:S(2)}) async-start(bf16[8,144,64]{1,2,0:T(8,128)(2,1)} %copy.12), calls=%async_computation | async-start | bytes 524288 | tf_op jit(solution)/shard_map/all_to_all | solution.py:26
Sparse Core Ops, SparseCore 0:
  13.8 102.3 all-gather.3
